TPU v7x, 32 devices: a whole 2x2x4 slice. The times are simulated.
32 devices in a mesh: pi: 4 (over y, x), pj: 8 (over z, core).
Axes of the slice: x: 2, y: 2, z: 4, core: 2. Of those that a mesh axis runs over, the one named last changes fastest.
Arguments:
- duo_embedding: bfloat16 [1024, 1024, 128], P('pi', 'pj'), may hold values from -12 to 12
- duo_attention_weights: float32 [128, 8], replicated, may hold values from -16 to 16
- aligned_embedding: bfloat16 [256, 64, 1024], P('pj', None, 'pi'), may hold values from -6 to 6
- aligned_scaling_weights: float32 [64], replicated, may hold values from 0.5 to 1.5
- aligned_shift_vector: float32 [64], replicated, may hold values from -3 to 3
- payload_weights: bfloat16 [64, 256], replicated, may hold values from -0.75 to 0.75
- switch_weights: bfloat16 [64, 256], replicated, may hold values from -0.75 to 0.75
- closing_weights: bfloat16 [256, 64], replicated, may hold values from -1.5 to 1.5
Outputs:
- update: bfloat16 [256, 64, 1024], P('pj', None, 'pi')
All inputs are finite; a program needn't handle non-finite values.
Results may differ from a plain program's by a relative error of at most 0.009.
Values may be sent and summed in bfloat16 or wider, within the bound.
A program may use at most 192 MiB of HBM per device.

v0:
```python
import jax
import jax.numpy as jnp
from jax import lax
from jax.sharding import PartitionSpec as P

EPS = 1e-05


def rescale_embedding(inputs, axis):
    row_mean = jnp.mean(inputs, axis=axis, keepdims=True)
    centred = inputs - row_mean
    variance = jnp.mean(centred * centred, axis=axis, keepdims=True)
    return centred * lax.rsqrt(variance + EPS)


def body(
    duo_embedding,
    duo_attention_weights,
    aligned_embedding,
    aligned_scaling_weights,
    aligned_shift_vector,
    payload_weights,
    switch_weights,
    closing_weights,
):
    attender_tally = duo_attention_weights.shape[1]
    entry_tally = duo_embedding.shape[0]
    aligned_seq_tally = aligned_embedding.shape[0]
    inner_embed_size = payload_weights.shape[1]
    attender_span = inner_embed_size // attender_tally
    pair_normed = rescale_embedding(duo_embedding.astype(jnp.float32), 2)
    scores = jnp.einsum(
        "ijc,ch->hij", pair_normed, duo_attention_weights, precision=lax.Precision.HIGHEST
    )
    row_peak = lax.pmax(jnp.max(scores, axis=2), "pj")
    exp_scores = jnp.exp(scores - row_peak[:, :, None]).astype(jnp.bfloat16)
    row_total = lax.psum(jnp.sum(exp_scores, axis=2, dtype=jnp.float32), "pj")
    weights_full = lax.all_gather(exp_scores, "pj", axis=2, tiled=True)
    rescaled_aligned = (
        rescale_embedding(aligned_embedding.astype(jnp.float32), 1)
        * aligned_scaling_weights[None, :, None]
        + aligned_shift_vector[None, :, None]
    ).astype(jnp.bfloat16)
    switch_share = jax.nn.sigmoid(
        jnp.einsum(
            "scn,ce->sen", rescaled_aligned, switch_weights, preferred_element_type=jnp.float32
        )
    )
    value_segment = jnp.einsum(
        "scn,ce->sen",
        lax.all_gather(rescaled_aligned, "pi", axis=2, tiled=True),
        payload_weights,
        preferred_element_type=jnp.float32,
    ).astype(jnp.bfloat16)
    piece_span = value_segment.shape[2]
    payload_each_attender = value_segment.reshape(
        aligned_seq_tally, attender_tally, attender_span, piece_span
    )
    numerator = jnp.einsum(
        "hij,shcj->shci", weights_full, payload_each_attender, preferred_element_type=jnp.float32
    )
    gate_per_head = switch_share.reshape(
        aligned_seq_tally, attender_tally, attender_span, entry_tally
    )
    averaged_result = (gate_per_head * (numerator / row_total[None, :, None, :])).astype(
        jnp.bfloat16
    )
    averaged_result = averaged_result.reshape(aligned_seq_tally, inner_embed_size, entry_tally)
    return jnp.einsum(
        "ser,ec->scr", averaged_result, closing_weights, preferred_element_type=jnp.float32
    ).astype(jnp.bfloat16)


def solution(mesh):
    return jax.shard_map(
        body,
        mesh=mesh,
        in_specs=(P("pi", "pj", None), P(), P("pj", None, "pi"), P(), P(), P(), P(), P()),
        out_specs=P("pj", None, "pi"),
        check_vma=False,
    )
```

profile of v0, /device:TPU:0, one launch (start us, length us, event | category | flops | bytes accessed | tf_op | source)
XLA Modules:
  0.0 166.8 jit_solution(10398905157669121667)
XLA Ops:
  6.5 0.0 copy-start
  6.5 0.0 all-gather.3.cloned.1.call-start
  6.5 1.4 convert_reduce_fusion.1
  8.0 1.6 fusion.17
  9.6 2.7 %fusion.20 = bf16[32,64,256]{2,1,0:T(8,128)(2,1)} fusion(bf16[32,64,256]{2,1,0:T(8,128)(2,1)} %param.10, f32[64]{0:T(128)} %param.12, f32[64]{0:T(128)} %param.11, f32[32,256]{1,0:T(8,128)S(1)} %add_rsqrt_fusion.1, f32[32,256]{1,0:T(8,128)S(1)} %broadcast_multiply_fusion.1), kind=kLoop, calls=%fused_computation.22 | loop fusion | flops 3145728 | bytes 2163200 | tf_op jit(solution)/shard_map/convert_element_type | solution.py:43
  12.3 0.0 all-gather.3.cloned.1.call-update
  12.4 0.0 copy-start.4
  12.4 0.0 all-gather.5.cloned.1.call-start
  12.4 0.0 slice-start
  12.4 5.8 %convert_reduce_fusion = f32[256,128]{1,0:T(8,128)S(1)} fusion(bf16[256,128,128]{2,1,0:T(8,128)(2,1)} %param.8), kind=kLoop, calls=%fused_computation.1 | loop fusion | flops 8355840 | bytes 8519680 | tf_op jit(solution)/shard_map/reduce_sum | solution.py:10
  18.3 0.0 slice-start.1
  18.3 10.9 %fusion.2 = f32[256,128]{1,0:T(8,128)S(1)} fusion(bf16[256,128,128]{2,1,0:T(8,128)(2,1)} %param.8, f32[256,128]{1,0:T(8,128)S(1)} %broadcast_multiply_fusion), kind=kLoop, calls=%fused_computation.4 | loop fusion | flops 16744448 | bytes 8650752 | tf_op jit(solution)/shard_map/reduce_sum | solution.py:12
  29.2 0.0 copy-done.4
  29.2 0.0 slice-done
  29.2 0.0 slice-done.1
  29.2 0.0 copy-start.1
  29.2 0.0 copy-start.3
  29.2 31.4 %fusion.29 = (f32[8,256]{0,1:T(8,128)S(1)}, f32[8,256,128]{2,0,1:T(8,128)S(1)}) fusion(f32[128,8]{0,1:T(8,128)S(1)} %copy-done.4, bf16[256,128,128]{2,1,0:T(8,128)(2,1)S(1)} %bitcast.34, f32[256,128]{1,0:T(8,128)S(1)} %add_rsqrt_fusion, f32[256,128]{1,0:T(8,128)S(1)} %broadcast_multiply_fusion), kind=kOutput, calls=%fused_computation.36 | convolution fusion | flops 415496192 | bytes 9711616 | tf_op jit(solution)/shard_map/ijc,ch->hij/dot_general | solution.py:32
  60.6 31.8 %pmax.7 = f32[8,256]{0,1:T(8,128)S(1)} all-reduce(f32[8,256]{0,1:T(8,128)S(1)} %get-tuple-element.7), channel_id=1, replica_groups=mesh['pi'=4,'pj'=8] {'pj'}, use_global_device_ids=true, to_apply=%region_5.0 | all-reduce | flops 2048 | bytes 16384 | tf_op jit(solution)/shard_map/pmax | solution.py:35
  92.4 1.2 convert_reduce_fusion.2
  93.6 0.0 all-gather.5.cloned.1.call-update
  93.6 30.4 %psum.7 = f32[8,256]{0,1:T(8,128)S(1)} all-reduce(f32[8,256]{0,1:T(8,128)S(1)} %get-tuple-element.5), channel_id=1, replica_groups=mesh['pi'=4,'pj'=8] {'pj'}, use_global_device_ids=true, to_apply=%region_7.0 | all-reduce | flops 2048 | bytes 16384 | tf_op jit(solution)/shard_map/psum | solution.py:37
  124.0 0.1 copy.18
  124.0 0.0 copy-done.1
  124.0 0.0 copy-done.3
  124.0 5.9 %add_divide_fusion = f32[32,256,256]{1,2,0:T(8,128)} fusion(bf16[32,64,256]{2,1,0:T(8,128)(2,1)S(1)} %copy-done.1, bf16[64,256]{1,0:T(8,128)(2,1)S(1)} %copy-done.3), kind=kOutput, calls=%fused_computation.13 | convolution fusion | flops 274726912 | bytes 9469952 | tf_op jit(solution)/shard_map/scn,ce->sen/dot_general | solution.py:45
  130.0 0.0 copy-done
  130.0 10.8 %convolution_convert_fusion = bf16[32,1024,256]{1,2,0:T(8,128)(2,1)} fusion(bf16[32,64,1024]{2,1,0:T(8,128)(2,1)} %all-gather.3.cloned.1.call-done, bf16[64,256]{1,0:T(8,128)(2,1)S(1)} %copy-done), kind=kOutput, calls=%fused_computation.8 | convolution fusion | flops 1082130432 | bytes 21004288 | tf_op jit(solution)/shard_map/scn,ce->sen/dot_general | solution.py:49
  140.8 0.3 all-gather.5.cloned.1.call-done
  141.1 14.4 %fusion.7 = bf16[32,8,32,256]{3,2,0,1:T(8,128)(2,1)} fusion(f32[32,8,32,256]{3,2,1,0:T(8,128)} %bitcast.38, f32[8,256]{1,0:T(8,128)S(1)} %copy.18, bf16[8,256,1024,1]{2,0,1,3:T(8,128)(2,1)} %bitcast.37, bf16[32,8,32,1024]{3,2,1,0:T(8,128)(2,1)} %bitcast.35), kind=kOutput, calls=%fused_computation.10 | convolution fusion | flops 4301258752 | bytes 33562624 | tf_op jit(solution)/shard_map/hij,shcj->shci/dot_general | solution.py:59
  155.5 2.6 %copy.20 = bf16[32,8,32,256]{3,2,1,0:T(8,128)(2,1)S(1)} copy(bf16[32,8,32,256]{3,2,0,1:T(8,128)(2,1)} %fusion.7) | data formatting | bytes 8388608 | tf_op jit(solution)/shard_map/convert_element_type | solution.py:65
  158.1 1.8 %fusion.21 = bf16[32,64,256]{2,1,0:T(8,128)(2,1)} fusion(bf16[32,256,256]{2,1,0:T(8,128)(2,1)S(1)} %bitcast.36, bf16[256,64]{0,1:T(8,128)(2,1)S(1)} %copy-done.2), kind=kOutput, calls=%fused_computation.24 | convolution fusion | flops 268959744 | bytes 5275648 | tf_op jit(solution)/shard_map/ser,ec->scr/dot_general | solution.py:69
  (8 shorter events, 0.1 us)
Async XLA Ops:
  6.5 123.4 %copy-start = (bf16[64,256]{1,0:T(8,128)(2,1)S(1)}, bf16[64,256]{1,0:T(8,128)(2,1)}, u32[]{:S(2)}) copy-start(bf16[64,256]{1,0:T(8,128)(2,1)} %param.13) | copy-start | bytes 98308
  6.5 123.4 %all-gather.3.cloned.1.call-start = ((), (), s32[]{:S(2)}) async-start(), calls=%async_computation | async-start | bytes 5242880 | tf_op jit(solution)/shard_map/all_gather | solution.py:51
  12.4 16.8 %copy-start.4 = (f32[128,8]{0,1:T(8,128)S(1)}, f32[128,8]{0,1:T(8,128)}, u32[]{:S(2)}) copy-start(f32[128,8]{0,1:T(8,128)} %param.9) | copy-start | bytes 12292
  12.4 128.7 %all-gather.5.cloned.1.call-start = ((), (), s32[]{:S(2)}) async-start(), calls=%async_computation.1 | async-start | bytes 4718592 | tf_op jit(solution)/shard_map/all_gather | solution.py:38
  12.4 16.8 %slice-start = ((s8[8388608]{0:T(1024)(128)(4,1)}), s8[4194304]{0:T(1024)(128)(4,1)S(1)}, s32[]{:S(2)}) async-start(s8[8388608]{0:T(1024)(128)(4,1)} %bitcast.33), calls=%async_computation.2 | async-start | bytes 8388608
  18.3 10.9 %slice-start.1 = ((s8[8388608]{0:T(1024)(128)(4,1)}), s8[4194304]{0:T(1024)(128)(4,1)S(1)}, s32[]{:S(2)}) async-start(s8[8388608]{0:T(1024)(128)(4,1)} %bitcast.33), calls=%async_computation.3 | async-start | bytes 8388608
  29.2 94.8 %copy-start.1 = (bf16[32,64,256]{2,1,0:T(8,128)(2,1)S(1)}, bf16[32,64,256]{2,1,0:T(8,128)(2,1)}, u32[]{:S(2)}) copy-start(bf16[32,64,256]{2,1,0:T(8,128)(2,1)} %fusion.20) | copy-start | bytes 3145732
  29.2 94.8 %copy-start.3 = (bf16[64,256]{1,0:T(8,128)(2,1)S(1)}, bf16[64,256]{1,0:T(8,128)(2,1)}, u32[]{:S(2)}) copy-start(bf16[64,256]{1,0:T(8,128)(2,1)} %param.14) | copy-start | bytes 98308
  155.5 2.6 %copy-start.2 = (bf16[256,64]{0,1:T(8,128)(2,1)S(1)}, bf16[256,64]{0,1:T(8,128)(2,1)}, u32[]{:S(2)}) copy-start(bf16[256,64]{0,1:T(8,128)(2,1)} %param.15) | copy-start | bytes 98308
Sparse Core Ops, SparseCore 0:
  12.5 55.1 all-gather.2
  93.7 47.3 all-gather.4
where the time goes:
time: 167 us
  matrix products  64.4 us (39%)
  blocking collectives  62.1 us (37%)
  other arithmetic  23.6 us (14%)
  between operations  13.6 us (8%)
  local copies, waits for them, and re-layouts  2.73 us (2%)
    pmax x1, blocking collectives, body(): row_peak = lax.pmax(jnp.max(scores, axis=2), 'pj')  31.8 us
    dot_general x1, matrix products, body(): jnp.einsum('ijc,ch->hij', pair_normed, duo_attention_weights, precision=l...  31.4 us
    psum x1, blocking collectives, body(): row_total = lax.psum(jnp.sum(exp_scores, axis=2, dtype=jnp.float32), 'pj')  30.4 us
    dot_general x1, matrix products, body(): jnp.einsum('hij,shcj->shci', weights_full, payload_each_attender, preferr...  14.4 us
    reduce_sum x2, other arithmetic, rescale_embedding(): variance = jnp.mean(centred * centred, axis=axis, keepdims=True)  12.5 us
    dot_general x1, matrix products, body(): jnp.einsum('scn,ce->sen', lax.all_gather(rescaled_aligned, 'pi', axis=2,...  10.8 us
    reduce_sum x2, other arithmetic, rescale_embedding(): row_mean = jnp.mean(inputs, axis=axis, keepdims=True)  7.24 us
    dot_general x1, matrix products, body(): jnp.einsum('scn,ce->sen', rescaled_aligned, switch_weights, preferred_ele...  5.93 us
  transfers between devices with their start and end apart: 2, of which 1 were waited for; matrix products, arithmetic and copies ran while one was open for 40% of the time, Pallas kernels for 0%

commit v1 on v0

--- a/solution.py
+++ b/solution.py
@@ -34,7 +34,7 @@
     )
     row_peak = lax.pmax(jnp.max(scores, axis=2), "pj")
     exp_scores = jnp.exp(scores - row_peak[:, :, None]).astype(jnp.bfloat16)
-    row_total = lax.psum(jnp.sum(exp_scores, axis=2, dtype=jnp.float32), "pj")
+    row_total = jnp.sum(jax.lax.all_gather(jnp.sum(exp_scores, axis=2, dtype=jnp.float32), "pj"), 0)
     weights_full = lax.all_gather(exp_scores, "pj", axis=2, tiled=True)
     rescaled_aligned = (
         rescale_embedding(aligned_embedding.astype(jnp.float32), 1)

time: 167 us -> 166 us (level)
  blocking collectives: 62.1 us -> 46.1 us
  waiting for transfers between devices: 0.32 us -> 14.9 us
    psum x1 -> x0, blocking collectives: 30.4 us -> none  [body(): row_total = lax.psum(jnp.sum(exp_scores, axis=2, dtype=jnp.float32), 'pj')]
    all_gather x1, waiting for transfers between devices: 0.29 us -> 14.8 us  [body(): weights_full = lax.all_gather(exp_scores, 'pj', axis=2, tiled=True)]
    all_gather x0 -> x1, blocking collectives: none -> 14.4 us  [body(): jax.lax.all_gather(jnp.sum(exp_scores, axis=2, dtype=jnp.float32), 'pj')]
where the time goes in v1:
time: 166 us; the launch traced here: 165 us
  matrix products  64.3 us (39%)
  blocking collectives  46.1 us (28%)
  other arithmetic  23.6 us (14%)
  waiting for transfers between devices  14.9 us (9%)
  between operations  13.6 us (8%)
  local copies, waits for them, and re-layouts  2.73 us (2%)
    pmax x1, blocking collectives, body(): row_peak = lax.pmax(jnp.max(scores, axis=2), 'pj')  31.8 us
    dot_general x1, matrix products, body(): jnp.einsum('ijc,ch->hij', pair_normed, duo_attention_weights, precision=l...  31.4 us
    all_gather x1, waiting for transfers between devices, body(): weights_full = lax.all_gather(exp_scores, 'pj', axis=2, tiled=True)  14.8 us
    dot_general x1, matrix products, body(): jnp.einsum('hij,shcj->shci', weights_full, payload_each_attender, preferr...  14.4 us
    all_gather x1, blocking collectives, body(): jax.lax.all_gather(jnp.sum(exp_scores, axis=2, dtype=jnp.float32), 'pj')  14.4 us
    reduce_sum x2, other arithmetic, rescale_embedding(): variance = jnp.mean(centred * centred, axis=axis, keepdims=True)  12.5 us
    dot_general x1, matrix products, body(): jnp.einsum('scn,ce->sen', lax.all_gather(rescaled_aligned, 'pi', axis=2,...  10.8 us
    reduce_sum x2, other arithmetic, rescale_embedding(): row_mean = jnp.mean(inputs, axis=axis, keepdims=True)  7.24 us
  transfers between devices with their start and end apart: 2, of which 1 were waited for; matrix products, arithmetic and copies ran while one was open for 40% of the time, Pallas kernels for 0%

profile of v1, /device:TPU:0, one launch (start us, length us, event | category | flops | bytes accessed | tf_op | source)
XLA Modules:
  0.0 165.3 jit_solution(1883269506123242119)
XLA Ops:
  6.5 0.0 copy-start
  6.5 0.0 all-gather.4.cloned.1.call-start
  6.5 1.4 convert_reduce_fusion.1
  8.0 1.6 fusion.17
  9.6 2.7 %fusion.20 = bf16[32,64,256]{2,1,0:T(8,128)(2,1)} fusion(bf16[32,64,256]{2,1,0:T(8,128)(2,1)} %param.10, f32[64]{0:T(128)} %param.12, f32[64]{0:T(128)} %param.11, f32[32,256]{1,0:T(8,128)S(1)} %add_rsqrt_fusion.1, f32[32,256]{1,0:T(8,128)S(1)} %broadcast_multiply_fusion.1), kind=kLoop, calls=%fused_computation.22 | loop fusion | flops 3145728 | bytes 2163200 | tf_op jit(solution)/shard_map/convert_element_type | solution.py:43
  12.3 0.0 all-gather.4.cloned.1.call-update
  12.4 0.0 copy-start.4
  12.4 0.0 all-gather.6.cloned.1.call-start
  12.4 0.0 slice-start
  12.4 5.8 %convert_reduce_fusion = f32[256,128]{1,0:T(8,128)S(1)} fusion(bf16[256,128,128]{2,1,0:T(8,128)(2,1)} %param.8), kind=kLoop, calls=%fused_computation.1 | loop fusion | flops 8355840 | bytes 8519680 | tf_op jit(solution)/shard_map/reduce_sum | solution.py:10
  18.3 0.0 slice-start.1
  18.3 10.9 %fusion.2 = f32[256,128]{1,0:T(8,128)S(1)} fusion(bf16[256,128,128]{2,1,0:T(8,128)(2,1)} %param.8, f32[256,128]{1,0:T(8,128)S(1)} %broadcast_multiply_fusion), kind=kLoop, calls=%fused_computation.4 | loop fusion | flops 16744448 | bytes 8650752 | tf_op jit(solution)/shard_map/reduce_sum | solution.py:12
  29.2 0.0 copy-done.4
  29.2 0.0 slice-done
  29.2 0.0 slice-done.1
  29.2 0.0 copy-start.1
  29.2 0.0 copy-start.3
  29.2 31.4 %fusion.29 = (f32[8,256]{0,1:T(8,128)S(1)}, f32[8,256,128]{2,0,1:T(8,128)S(1)}) fusion(f32[128,8]{0,1:T(8,128)S(1)} %copy-done.4, bf16[256,128,128]{2,1,0:T(8,128)(2,1)S(1)} %bitcast.36, f32[256,128]{1,0:T(8,128)S(1)} %add_rsqrt_fusion, f32[256,128]{1,0:T(8,128)S(1)} %broadcast_multiply_fusion), kind=kOutput, calls=%fused_computation.37 | convolution fusion | flops 415496192 | bytes 9711616 | tf_op jit(solution)/shard_map/ijc,ch->hij/dot_general | solution.py:32
  60.6 31.8 %pmax.7 = f32[8,256]{0,1:T(8,128)S(1)} all-reduce(f32[8,256]{0,1:T(8,128)S(1)} %get-tuple-element.7), channel_id=1, replica_groups=mesh['pi'=4,'pj'=8] {'pj'}, use_global_device_ids=true, to_apply=%region_5.0 | all-reduce | flops 2048 | bytes 16384 | tf_op jit(solution)/shard_map/pmax | solution.py:35
  92.4 1.2 convert_reduce_fusion.2
  93.6 0.0 all-gather.6.cloned.1.call-update
  93.6 0.1 copy.27
  93.6 14.4 %all-gather = f32[64,256]{1,0:T(8,128)S(1)} all-gather(f32[8,256]{1,0:T(8,128)S(1)} %copy.27), channel_id=2, replica_groups=mesh['pi'=4,'pj'=8] {'pj'}, dimensions={0}, use_global_device_ids=true | all-gather | bytes 73728 | tf_op jit(solution)/shard_map/all_gather | solution.py:37
  108.0 0.0 copy-done.1
  108.0 5.9 %add_divide_fusion = f32[32,256,256]{1,2,0:T(8,128)} fusion(bf16[32,64,256]{2,1,0:T(8,128)(2,1)S(1)} %copy-done.1, bf16[64,256]{1,0:T(8,128)(2,1)S(1)} %copy-done.3), kind=kOutput, calls=%fused_computation.13 | convolution fusion | flops 274726912 | bytes 9469952 | tf_op jit(solution)/shard_map/scn,ce->sen/dot_general | solution.py:45
  114.0 0.0 copy-done
  114.0 10.8 %convolution_convert_fusion = bf16[32,1024,256]{1,2,0:T(8,128)(2,1)} fusion(bf16[32,64,1024]{2,1,0:T(8,128)(2,1)} %all-gather.4.cloned.1.call-done, bf16[64,256]{1,0:T(8,128)(2,1)S(1)} %copy-done), kind=kOutput, calls=%fused_computation.8 | convolution fusion | flops 1082130432 | bytes 21004288 | tf_op jit(solution)/shard_map/scn,ce->sen/dot_general | solution.py:49
  124.8 14.8 %all-gather.6.cloned.1.call-done = bf16[8,256,1024]{2,0,1:T(8,128)(2,1)} async-done(((bf16[8,256,128]{2,0,1:T(8,128)(2,1)}), bf16[8,256,1024]{2,0,1:T(8,128)(2,1)}) %all-gather.6.cloned.1.call-update) | async-done | bytes 4194320 | tf_op jit(solution)/shard_map/all_gather | solution.py:38
  139.6 14.4 %fusion.7 = bf16[32,8,32,256]{3,2,0,1:T(8,128)(2,1)} fusion(f32[32,8,32,256]{3,2,1,0:T(8,128)} %bitcast.40, f32[8,256]{1,0:T(8,128)S(1)} %bitcast_reduce_fusion, bf16[8,256,1024,1]{2,0,1,3:T(8,128)(2,1)} %bitcast.39, bf16[32,8,32,1024]{3,2,1,0:T(8,128)(2,1)} %bitcast.37), kind=kOutput, calls=%fused_computation.10 | convolution fusion | flops 4301258752 | bytes 33562624 | tf_op jit(solution)/shard_map/hij,shcj->shci/dot_general | solution.py:59
  154.0 2.6 %copy.29 = bf16[32,8,32,256]{3,2,1,0:T(8,128)(2,1)S(1)} copy(bf16[32,8,32,256]{3,2,0,1:T(8,128)(2,1)} %fusion.7) | data formatting | bytes 8388608 | tf_op jit(solution)/shard_map/convert_element_type | solution.py:65
  156.6 0.0 copy-done.2
  156.7 1.8 %fusion.21 = bf16[32,64,256]{2,1,0:T(8,128)(2,1)} fusion(bf16[32,256,256]{2,1,0:T(8,128)(2,1)S(1)} %bitcast.38, bf16[256,64]{0,1:T(8,128)(2,1)S(1)} %copy-done.2), kind=kOutput, calls=%fused_computation.24 | convolution fusion | flops 268959744 | bytes 5275648 | tf_op jit(solution)/shard_map/ser,ec->scr/dot_general | solution.py:69
  (9 shorter events, 0.1 us)
Async XLA Ops:
  6.5 107.4 %copy-start = (bf16[64,256]{1,0:T(8,128)(2,1)S(1)}, bf16[64,256]{1,0:T(8,128)(2,1)}, u32[]{:S(2)}) copy-start(bf16[64,256]{1,0:T(8,128)(2,1)} %param.13) | copy-start | bytes 98308
  6.5 107.4 %all-gather.4.cloned.1.call-start = ((), (), s32[]{:S(2)}) async-start(), calls=%async_computation | async-start | bytes 5242880 | tf_op jit(solution)/shard_map/all_gather | solution.py:51
  12.4 16.8 %copy-start.4 = (f32[128,8]{0,1:T(8,128)S(1)}, f32[128,8]{0,1:T(8,128)}, u32[]{:S(2)}) copy-start(f32[128,8]{0,1:T(8,128)} %param.9) | copy-start | bytes 12292
  12.4 127.2 %all-gather.6.cloned.1.call-start = ((), (), s32[]{:S(2)}) async-start(), calls=%async_computation.1 | async-start | bytes 4718592 | tf_op jit(solution)/shard_map/all_gather | solution.py:38
  12.4 16.8 %slice-start = ((s8[8388608]{0:T(1024)(128)(4,1)}), s8[4194304]{0:T(1024)(128)(4,1)S(1)}, s32[]{:S(2)}) async-start(s8[8388608]{0:T(1024)(128)(4,1)} %bitcast.35), calls=%async_computation.2 | async-start | bytes 8388608
  18.3 10.9 %slice-start.1 = ((s8[8388608]{0:T(1024)(128)(4,1)}), s8[4194304]{0:T(1024)(128)(4,1)S(1)}, s32[]{:S(2)}) async-start(s8[8388608]{0:T(1024)(128)(4,1)} %bitcast.35), calls=%async_computation.3 | async-start | bytes 8388608
  29.2 78.8 %copy-start.1 = (bf16[32,64,256]{2,1,0:T(8,128)(2,1)S(1)}, bf16[32,64,256]{2,1,0:T(8,128)(2,1)}, u32[]{:S(2)}) copy-start(bf16[32,64,256]{2,1,0:T(8,128)(2,1)} %fusion.20) | copy-start | bytes 3145732
  29.2 78.8 %copy-start.3 = (bf16[64,256]{1,0:T(8,128)(2,1)S(1)}, bf16[64,256]{1,0:T(8,128)(2,1)}, u32[]{:S(2)}) copy-start(bf16[64,256]{1,0:T(8,128)(2,1)} %param.14) | copy-start | bytes 98308
  154.0 2.6 %copy-start.2 = (bf16[256,64]{0,1:T(8,128)(2,1)S(1)}, bf16[256,64]{0,1:T(8,128)(2,1)}, u32[]{:S(2)}) copy-start(bf16[256,64]{0,1:T(8,128)(2,1)} %param.15) | copy-start | bytes 98308
Sparse Core Ops, SparseCore 0:
  12.5 55.1 all-gather.3
  93.7 45.8 all-gather.5
